TPU v7x, 32 devices: a whole 2x2x4 slice. The times are simulated.
32 devices in a mesh: mem: 8 (over z, x), chan: 4 (over y, core).
Axes of the slice: x: 2, y: 2, z: 4, core: 2. Of those that a mesh axis runs over, the one named last changes fastest.
Arguments:
- state_anom: bfloat16 [8, 64, 137], P(None, 'mem'), may hold values from -6 to 6
- radiance_anom: bfloat16 [8, 64, 8704], P(None, 'mem', 'chan'), may hold values from -6 to 6
- inv_noise: float32 [8704], P('chan'), may hold values from 0.02 to 0.2
- innovation: float32 [8, 8704], P(None, 'chan'), may hold values from -6 to 6
- valid_count: int32 [8], replicated, may hold values from 4352 to 8461
Outputs:
- information: float32 [8, 137, 137], P('mem')
- gradient: float32 [8, 137], P('mem')
- increment: float32 [8, 137], P('mem')
All inputs are finite; a program needn't handle non-finite values.
Results may differ from a plain program's by a relative error of at most 0.0003.
Values may be sent and summed in bfloat16 or wider, within the bound.
A program may use at most 64 MiB of HBM per device.

v0:
```python
import jax
import jax.numpy as jnp
from jax import lax
from jax.sharding import PartitionSpec as P


def slab_terms(cross, weight, innov_rows):
    weighted = cross * weight[:, :, None]
    info_part = jnp.einsum("pcs,pct->pst", weighted, cross, precision=lax.Precision.HIGHEST)
    grad_part = jnp.einsum("pcs,pc->ps", weighted, innov_rows, precision=lax.Precision.HIGHEST)
    return (info_part, grad_part)


def shards(state_anom, radiance_anom, inv_noise, innovation, valid_count):
    profiles = state_anom.shape[0]
    states = state_anom.shape[2]
    slab_width = radiance_anom.shape[2]
    members_all = state_anom.shape[1] * lax.axis_size("mem")
    prof_local = profiles // lax.axis_size("mem")
    slab_start = lax.axis_index("chan") * slab_width
    own_rad, own_states = (
        lax.all_to_all(radiance_anom, "mem", split_axis=0, concat_axis=1, tiled=True),
        lax.all_to_all(state_anom, "mem", split_axis=0, concat_axis=1, tiled=True),
    )
    cross = jnp.einsum("pmc,pms->pcs", own_rad, own_states, preferred_element_type=jnp.float32)
    cross = cross / jnp.float32(members_all - 1)
    first_prof = lax.axis_index("mem") * prof_local
    own_count = lax.dynamic_slice_in_dim(valid_count, first_prof, prof_local, 0)
    slots = slab_start + jnp.arange(slab_width, dtype=jnp.int32)
    valid = (slots[None, :] < own_count[:, None]).astype(jnp.float32)
    weight = inv_noise[None, :] * valid
    innov_rows = lax.dynamic_slice_in_dim(innovation, first_prof, prof_local, 0)
    info_share, grad_share = slab_terms(cross, weight, innov_rows)
    information, gradient = lax.psum((info_share, grad_share), "chan")
    system = information + jnp.eye(states, dtype=jnp.float32)[None]
    factor = jnp.linalg.cholesky(system)
    increment = jax.scipy.linalg.cho_solve((factor, True), gradient[:, :, None])[:, :, 0]
    return (information, gradient, increment)


def solution(mesh):
    in_specs = (P(None, "mem", None), P(None, "mem", "chan"), P("chan"), P(None, "chan"), P())
    out_specs = (P("mem", None, None), P("mem", None), P("mem", None))
    return jax.shard_map(shards, mesh=mesh, in_specs=in_specs, out_specs=out_specs, check_vma=False)
```

profile of v0, /device:TPU:0, one launch (start us, length us, event | category | flops | bytes accessed | tf_op | source)
XLA Modules:
  0.0 121.7 jit_solution(8152377795422508364)
XLA Ops:
  7.2 14.1 %all_to_all.8 = bf16[8,8,137]{2,1,0:T(8,128)(2,1)S(1)} all-to-all(bf16[8,8,137]{2,1,0:T(8,128)(2,1)} %param.5), channel_id=1, replica_groups=mesh['mem'=8,'chan'=4] {'mem'}, dimensions={0} | all-to-all | bytes 35072 | tf_op jit(solution)/shard_map/all_to_all | solution.py:23
  21.3 3.4 %all-to-all-start = ((bf16[8,8,2176]{2,1,0:T(8,128)(2,1)}), bf16[8,8,2176]{2,1,0:T(8,128)(2,1)S(1)}, u32[]{:S(2)}, u32[]{:S(2)}) async-start(bf16[8,8,2176]{2,1,0:T(8,128)(2,1)} %param.6), calls=%async_computation | async-start | bytes 557056 | tf_op jit(solution)/shard_map/all_to_all | solution.py:22
  24.7 0.0 all-reduce.5.cloned.1.call-start
  24.8 1.2 %dynamic_slice.6 = s32[1]{0:T(128)} dynamic-slice(s32[8]{0:T(128)} %param.9, s32[]{:T(128)S(6)} %select_n.8), dynamic_slice_sizes={1} | dynamic-slice | bytes 12 | tf_op jit(solution)/shard_map/dynamic_slice | solution.py:28
  26.1 1.4 %select_multiply_fusion = f32[2176]{0:T(1024)S(1)} fusion(f32[2176]{0:T(1024)} %param.7, s32[]{:T(128)} %bitcast.1, s32[]{:T(128)S(6)} %mul.19), kind=kLoop, calls=%fused_computation.43 | loop fusion | flops 8704 | bytes 17416 | tf_op jit(solution)/shard_map/mul | solution.py:8
  27.4 5.6 %all-to-all-done = bf16[8,8,2176]{2,1,0:T(8,128)(2,1)S(1)} async-done(((bf16[8,8,2176]{2,1,0:T(8,128)(2,1)}), bf16[8,8,2176]{2,1,0:T(8,128)(2,1)S(1)}, u32[]{:S(2)}, u32[]{:S(2)}) %all-to-all-start) | async-done | bytes 278560 | tf_op jit(solution)/shard_map/all_to_all | solution.py:22
  33.0 0.4 convolution_bitcast_fusion
  33.4 1.9 %fusion.5 = f32[1,137,137]{1,2,0:T(8,128)} fusion(f32[2176,137]{0,1:T(8,128)S(1)} %convolution_bitcast_fusion, f32[2176]{0:T(1024)S(1)} %select_multiply_fusion), kind=kOutput, calls=%fused_computation.6 | convolution fusion | flops 490692352 | bytes 1276228 | tf_op jit(solution)/shard_map/pcs,pct->pst/dot_general | solution.py:9
  35.3 0.0 all-reduce.5.cloned.1.call-update
  35.3 1.1 fusion.2
  36.5 5.8 %psum.15 = f32[1,137]{1,0:T(1,128)S(1)} all-reduce(f32[1,137]{1,0:T(1,128)S(1)} %fusion.2), channel_id=1, replica_groups=mesh['mem'=8,'chan'=4] {'chan'}, use_global_device_ids=true, to_apply=%region_1.0 | all-reduce | flops 137 | bytes 1096 | tf_op jit(solution)/shard_map/psum | solution.py:34
  42.3 23.1 %all-reduce.5.cloned.1.call-done = f32[1,137,137]{1,2,0:T(8,128)} async-done(((f32[1,137,137]{1,2,0:T(8,128)}), f32[1,137,137]{1,2,0:T(8,128)}) %all-reduce.5.cloned.1.call-update) | async-done | bytes 75092 | tf_op jit(solution)/shard_map/psum | solution.py:34
  65.4 0.9 convert_add_fusion
  66.3 0.1 copy.9
  66.4 0.9 fusion.18
  67.4 11.7 %custom-call.20 = f32[1,128,128]{2,1,0:T(8,128)S(1)} custom-call(f32[1,128,128]{2,1,0:T(8,128)S(1)} %cholesky.123), custom_call_target="Cholesky" | custom-call | tf_op jit(solution)/shard_map/jit(cholesky)/cholesky | solution.py:36
  79.2 9.8 %custom-call.21 = f32[1,1,128,128]{2,3,1,0:T(8,128)S(1)} custom-call(f32[1,1,128,128]{3,2,1,0:T(8,128)S(1)} %get-tuple-element.27), custom_call_target="InvertDiagBlocksLowerTriangular" | custom-call | tf_op jit(solution)/shard_map/jit(cholesky)/cholesky | solution.py:36
  89.0 0.2 bitcast_dynamic-update-slice_fusion
  89.1 0.1 fusion.10
  89.3 0.8 custom-call.22
  90.1 0.7 compare_reduce_fusion.1
  90.8 0.6 compare_reduce_fusion
  92.7 0.1 fusion.19
  92.9 19.7 %custom-call.23 = f32[2,128,128]{1,2,0:T(8,128)S(1)} custom-call(f32[2,128,128]{2,1,0:T(8,128)S(1)} %pad_maximum_fusion), custom_call_target="InvertDiagBlocksLowerTriangular" | custom-call | tf_op jit(solution)/shard_map/jit(_cho_solve)/triangular_solve | solution.py:37
  112.5 0.2 fusion.22
  112.7 0.1 fusion.14
  112.8 0.1 convolution_bitcast_fusion.5
  113.0 0.1 convolution_bitcast_fusion.4
  113.1 0.1 fusion.12
  113.3 0.2 convolution_bitcast_fusion.2
  113.5 0.6 maximum_bitcast_fusion
  114.1 0.8 copy.11
  (15 shorter events, 0.2 us)
Async XLA Ops:
  7.2 28.2 %copy-start = (f32[8,2176]{1,0:T(8,128)S(1)}, f32[8,2176]{1,0:T(8,128)}, u32[]{:S(2)}) copy-start(f32[8,2176]{1,0:T(8,128)} %param.8) | copy-start | bytes 208900
  21.3 11.7 %all-to-all-start = ((bf16[8,8,2176]{2,1,0:T(8,128)(2,1)}), bf16[8,8,2176]{2,1,0:T(8,128)(2,1)S(1)}, u32[]{:S(2)}, u32[]{:S(2)}) async-start(bf16[8,8,2176]{2,1,0:T(8,128)(2,1)} %param.6), calls=%async_computation | async-start | bytes 557056 | tf_op jit(solution)/shard_map/all_to_all | solution.py:22
  24.7 40.7 %all-reduce.5.cloned.1.call-start = ((), (), s32[]{:S(2)}) async-start(), calls=%async_computation.2 | async-start | bytes 294912 | tf_op jit(solution)/shard_map/psum | solution.py:34
  42.3 70.4 %copy-start.2 = (f32[1,137]{1,0:T(1,128)}, f32[1,137]{1,0:T(1,128)S(1)}, u32[]{:S(2)}) copy-start(f32[1,137]{1,0:T(1,128)S(1)} %psum.15) | copy-start | bytes 1648
  66.3 47.8 %copy-start.1 = (f32[1,137,137]{1,2,0:T(8,128)S(1)}, f32[1,137,137]{1,2,0:T(8,128)}, u32[]{:S(2)}) copy-start(f32[1,137,137]{1,2,0:T(8,128)} %all-reduce.5.cloned.1.call-done) | copy-start | bytes 225232
Sparse Core Ops, SparseCore 0:
  35.5 29.8 all-reduce.4
where the time goes:
time: 122 us
  other arithmetic  47.4 us (39%)
  waiting for transfers between devices  28.7 us (24%)
  blocking collectives  19.9 us (16%)
  between operations  15.5 us (13%)
  matrix products  4.67 us (4%)
  starting transfers between devices  3.46 us (3%)
  local copies, waits for them, and re-layouts  2.15 us (2%)
    another operation x7, other arithmetic, shards(): factor = jnp.linalg.cholesky(system)  23.7 us
    psum x1, waiting for transfers between devices, shards(): information, gradient = lax.psum((info_share, grad_share), 'chan')  23.1 us
    another operation x6, other arithmetic, shards(): jax.scipy.linalg.cho_solve((factor, True), gradient[:, :, None])[:, :, 0]  19.8 us
    all_to_all x1, blocking collectives, shards(): lax.all_to_all(state_anom, 'mem', split_axis=0, concat_axis=1, tiled=True)  14.1 us
    psum x1, blocking collectives, shards(): information, gradient = lax.psum((info_share, grad_share), 'chan')  5.84 us
    all_to_all x1, waiting for transfers between devices, shards(): lax.all_to_all(radiance_anom, 'mem', split_axis=0, concat_axis=1, tiled=T...  5.57 us
    all_to_all x1, starting transfers between devices, shards(): lax.all_to_all(radiance_anom, 'mem', split_axis=0, concat_axis=1, tiled=T...  3.42 us
  transfers between devices with their start and end apart: 2, of which 2 were waited for; matrix products, arithmetic and copies ran while one was open for 3% of the time, Pallas kernels for 0%

commit v1 on v0

--- a/solution.py
+++ b/solution.py
@@ -2,6 +2,12 @@
 import jax.numpy as jnp
 from jax import lax
 from jax.sharding import PartitionSpec as P
+
+
+def trade_parts(array, axis, split, join):
+    pieces = jnp.split(array, lax.axis_size(axis), axis=split)
+    incoming = lax.all_to_all(jnp.stack(pieces), axis, 0, 0)
+    return jnp.concatenate(incoming, axis=join)
 
 
 def slab_terms(cross, weight, innov_rows):
@@ -19,7 +25,7 @@
     prof_local = profiles // lax.axis_size("mem")
     slab_start = lax.axis_index("chan") * slab_width
     own_rad, own_states = (
-        lax.all_to_all(radiance_anom, "mem", split_axis=0, concat_axis=1, tiled=True),
+        trade_parts(radiance_anom, "mem", 0, 1),
         lax.all_to_all(state_anom, "mem", split_axis=0, concat_axis=1, tiled=True),
     )
     cross = jnp.einsum("pmc,pms->pcs", own_rad, own_states, preferred_element_type=jnp.float32)

time: 122 us -> 130 us (1.066)
  blocking collectives: 19.9 us -> 5.87 us
  local copies, waits for them, and re-layouts: 2.15 us -> 13.2 us
  starting transfers between devices: 3.46 us -> 13.5 us
  waiting for transfers between devices: 28.7 us -> 30 us
    all_to_all x1 -> x0, blocking collectives: 14.1 us -> none  [shards(): lax.all_to_all(state_anom, 'mem', split_axis=0, concat_axis=1, tiled=True)]
    all_to_all x1 -> x2, starting transfers between devices: 3.42 us -> 13.4 us  [the longest x1 7.42 us: shards(): lax.all_to_all(state_anom, 'mem', split_axis=0, concat_axis=1, tiled=True)]
    unnamed x7 -> x16, local copies, waits for them, and re-layouts: 0.79 us -> 10.4 us
    another operation x0 -> x1, local copies, waits for them, and re-layouts: none -> 1.38 us  [trade_parts(): incoming = lax.all_to_all(jnp.stack(pieces), axis, 0, 0)]
    all_to_all x1 -> x2, waiting for transfers between devices: 5.57 us -> 6.77 us  [the longest x1 6.76 us: trade_parts(): incoming = lax.all_to_all(jnp.stack(pieces), axis, 0, 0)]
  transfers between devices with their start and end apart: 2 -> 3, of which waited for: 2 -> 2; matrix products, arithmetic and copies ran while one was open for 3% -> 11% of each run, Pallas kernels for 0% -> 0%
where the time goes in v1:
time: 130 us; the launch traced here: 129 us
  other arithmetic  46.6 us (36%)
  waiting for transfers between devices  30 us (23%)
  between operations  15.5 us (12%)
  starting transfers between devices  13.5 us (10%)
  local copies, waits for them, and re-layouts  13.2 us (10%)
  blocking collectives  5.87 us (5%)
  matrix products  4.66 us (4%)
    another operation x7, other arithmetic, shards(): factor = jnp.linalg.cholesky(system)  23.7 us
    psum x1, waiting for transfers between devices, shards(): information, gradient = lax.psum((info_share, grad_share), 'chan')  23.2 us
    another operation x6, other arithmetic, shards(): jax.scipy.linalg.cho_solve((factor, True), gradient[:, :, None])[:, :, 0]  19.8 us
    unnamed x16, local copies, waits for them, and re-layouts  10.4 us
    all_to_all x1, starting transfers between devices, shards(): lax.all_to_all(state_anom, 'mem', split_axis=0, concat_axis=1, tiled=True)  7.42 us
    all_to_all x1, waiting for transfers between devices, trade_parts(): incoming = lax.all_to_all(jnp.stack(pieces), axis, 0, 0)  6.76 us
    all_to_all x1, starting transfers between devices, trade_parts(): incoming = lax.all_to_all(jnp.stack(pieces), axis, 0, 0)  6 us
    psum x1, blocking collectives, shards(): information, gradient = lax.psum((info_share, grad_share), 'chan')  5.87 us
  transfers between devices with their start and end apart: 3, of which 2 were waited for; matrix products, arithmetic and copies ran while one was open for 11% of the time, Pallas kernels for 0%

profile of v1, /device:TPU:0, one launch (start us, length us, event | category | flops | bytes accessed | tf_op | source)
XLA Modules:
  0.0 129.3 jit_solution(3980842012712749811)
XLA Ops:
  7.2 7.4 %all-to-all-start.1 = ((bf16[8,8,137]{2,1,0:T(8,128)(2,1)}), bf16[8,8,137]{2,1,0:T(8,128)(2,1)S(1)}, u32[]{:S(2)}, u32[]{:S(2)}) async-start(bf16[8,8,137]{2,1,0:T(8,128)(2,1)} %param.5), calls=%async_computation.1 | async-start | bytes 65536 | tf_op jit(solution)/shard_map/all_to_all | solution.py:29
  14.6 1.4 %bitcast_dynamic-update-slice_fusion.7 = bf16[8,1,8,2176]{3,2,1,0:T(8,128)(2,1)} fusion(bf16[8,8,2176]{2,1,0:T(8,128)(2,1)} %param.6), kind=kLoop, calls=%fused_computation.51 | loop fusion | bytes 69632
  16.0 1.4 %bitcast_dynamic-update-slice_fusion.6 = bf16[8,1,8,2176]{3,2,1,0:T(8,128)(2,1)} fusion(bf16[8,1,8,2176]{3,2,1,0:T(8,128)(2,1)} %bitcast_dynamic-update-slice_fusion.7, bf16[8,8,2176]{2,1,0:T(8,128)(2,1)} %param.6), kind=kLoop, calls=%fused_computation.50 | loop fusion | bytes 69632
  17.4 1.4 %bitcast_dynamic-update-slice_fusion.5 = bf16[8,1,8,2176]{3,2,1,0:T(8,128)(2,1)} fusion(bf16[8,1,8,2176]{3,2,1,0:T(8,128)(2,1)} %bitcast_dynamic-update-slice_fusion.6, bf16[8,8,2176]{2,1,0:T(8,128)(2,1)} %param.6), kind=kLoop, calls=%fused_computation.49 | loop fusion | bytes 69632
  18.7 1.4 %bitcast_dynamic-update-slice_fusion.4 = bf16[8,1,8,2176]{3,2,1,0:T(8,128)(2,1)} fusion(bf16[8,1,8,2176]{3,2,1,0:T(8,128)(2,1)} %bitcast_dynamic-update-slice_fusion.5, bf16[8,8,2176]{2,1,0:T(8,128)(2,1)} %param.6), kind=kLoop, calls=%fused_computation.48 | loop fusion | bytes 69632
  20.1 1.4 %bitcast_dynamic-update-slice_fusion.3 = bf16[8,1,8,2176]{3,2,1,0:T(8,128)(2,1)} fusion(bf16[8,1,8,2176]{3,2,1,0:T(8,128)(2,1)} %bitcast_dynamic-update-slice_fusion.4, bf16[8,8,2176]{2,1,0:T(8,128)(2,1)} %param.6), kind=kLoop, calls=%fused_computation.47 | loop fusion | bytes 69632
  21.5 1.4 %bitcast_dynamic-update-slice_fusion.2 = bf16[8,1,8,2176]{3,2,1,0:T(8,128)(2,1)} fusion(bf16[8,1,8,2176]{3,2,1,0:T(8,128)(2,1)} %bitcast_dynamic-update-slice_fusion.3, bf16[8,8,2176]{2,1,0:T(8,128)(2,1)} %param.6), kind=kLoop, calls=%fused_computation.46 | loop fusion | bytes 69632
  22.9 1.4 %bitcast_dynamic-update-slice_fusion.1 = bf16[8,1,8,2176]{3,2,1,0:T(8,128)(2,1)} fusion(bf16[8,1,8,2176]{3,2,1,0:T(8,128)(2,1)} %bitcast_dynamic-update-slice_fusion.2, bf16[8,8,2176]{2,1,0:T(8,128)(2,1)} %param.6), kind=kLoop, calls=%fused_computation.45 | loop fusion | bytes 69632
  24.2 1.4 %bitcast_dynamic-update-slice_fusion = bf16[8,1,8,2176]{3,2,1,0:T(8,128)(2,1)} fusion(bf16[8,1,8,2176]{3,2,1,0:T(8,128)(2,1)} %bitcast_dynamic-update-slice_fusion.1, bf16[8,8,2176]{2,1,0:T(8,128)(2,1)} %param.6), kind=kLoop, calls=%fused_computation.44 | loop fusion | bytes 69632 | tf_op jit(solution)/shard_map/stack | solution.py:9
  25.6 6.0 %all-to-all-start = ((bf16[8,1,8,2176]{3,2,1,0:T(8,128)(2,1)}), bf16[8,1,8,2176]{3,2,1,0:T(8,128)(2,1)S(1)}, u32[]{:S(2)}, u32[]{:S(2)}) async-start(bf16[8,1,8,2176]{3,2,1,0:T(8,128)(2,1)} %bitcast_dynamic-update-slice_fusion), calls=%async_computation | async-start | bytes 557056 | tf_op jit(solution)/shard_map/all_to_all | solution.py:9
  31.7 1.2 dynamic_slice.6
  33.0 0.7 select_multiply_fusion
  33.6 6.8 %all-to-all-done = bf16[8,1,8,2176]{3,2,1,0:T(8,128)(2,1)S(1)} async-done(((bf16[8,1,8,2176]{3,2,1,0:T(8,128)(2,1)}), bf16[8,1,8,2176]{3,2,1,0:T(8,128)(2,1)S(1)}, u32[]{:S(2)}, u32[]{:S(2)}) %all-to-all-start) | async-done | bytes 278560 | tf_op jit(solution)/shard_map/all_to_all | solution.py:9
  40.4 0.4 fusion.18
  40.8 1.9 %fusion.5 = f32[1,137,137]{1,2,0:T(8,128)} fusion(f32[2176,137]{0,1:T(8,128)S(1)} %fusion.18, f32[2176]{0:T(1024)S(1)} %select_multiply_fusion), kind=kOutput, calls=%fused_computation.5 | convolution fusion | flops 490692352 | bytes 1276228 | tf_op jit(solution)/shard_map/pcs,pct->pst/dot_general | solution.py:15
  42.7 1.1 fusion.2
  43.9 5.9 %psum.15 = f32[1,137]{1,0:T(1,128)S(1)} all-reduce(f32[1,137]{1,0:T(1,128)S(1)} %fusion.2), channel_id=1, replica_groups=mesh['mem'=8,'chan'=4] {'chan'}, use_global_device_ids=true, to_apply=%region_1.0 | all-reduce | flops 137 | bytes 1096 | tf_op jit(solution)/shard_map/psum | solution.py:40
  49.8 23.2 %all-reduce.5.cloned.1.call-done = f32[1,137,137]{1,2,0:T(8,128)} async-done(((f32[1,137,137]{1,2,0:T(8,128)}), f32[1,137,137]{1,2,0:T(8,128)}) %all-reduce.5.cloned.1.call-update) | async-done | bytes 75092 | tf_op jit(solution)/shard_map/psum | solution.py:40
  73.0 0.9 convert_add_fusion
  74.0 0.9 fusion.20
  75.0 11.7 %custom-call.20 = f32[1,128,128]{2,1,0:T(8,128)S(1)} custom-call(f32[1,128,128]{2,1,0:T(8,128)S(1)} %cholesky.123), custom_call_target="Cholesky" | custom-call | tf_op jit(solution)/shard_map/jit(cholesky)/cholesky | solution.py:42
  86.8 9.8 %custom-call.21 = f32[1,1,128,128]{2,3,1,0:T(8,128)S(1)} custom-call(f32[1,1,128,128]{3,2,1,0:T(8,128)S(1)} %get-tuple-element.27), custom_call_target="InvertDiagBlocksLowerTriangular" | custom-call | tf_op jit(solution)/shard_map/jit(cholesky)/cholesky | solution.py:42
  96.6 0.2 bitcast_dynamic-update-slice_fusion.8
  96.9 0.8 custom-call.22
  97.6 0.7 compare_reduce_fusion.1
  98.4 0.6 compare_reduce_fusion
  100.4 19.7 %custom-call.23 = f32[2,128,128]{1,2,0:T(8,128)S(1)} custom-call(f32[2,128,128]{2,1,0:T(8,128)S(1)} %pad_maximum_fusion), custom_call_target="InvertDiagBlocksLowerTriangular" | custom-call | tf_op jit(solution)/shard_map/jit(_cho_solve)/triangular_solve | solution.py:43
  120.1 0.2 fusion.24
  120.7 0.1 fusion.12
  120.9 0.2 convolution_bitcast_fusion.1
  121.0 0.6 maximum_bitcast_fusion
  121.7 0.8 copy.11
  (26 shorter events, 1.0 us)
Async XLA Ops:
  7.2 35.6 %copy-start = (f32[8,2176]{1,0:T(8,128)S(1)}, f32[8,2176]{1,0:T(8,128)}, u32[]{:S(2)}) copy-start(f32[8,2176]{1,0:T(8,128)} %param.8) | copy-start | bytes 208900
  7.2 25.8 %copy-start.2 = (f32[2176]{0:T(1024)S(1)}, f32[2176]{0:T(1024)}, u32[]{:S(2)}) copy-start(f32[2176]{0:T(1024)} %param.7) | copy-start | bytes 26116
  7.2 18.4 %all-to-all-start.1 = ((bf16[8,8,137]{2,1,0:T(8,128)(2,1)}), bf16[8,8,137]{2,1,0:T(8,128)(2,1)S(1)}, u32[]{:S(2)}, u32[]{:S(2)}) async-start(bf16[8,8,137]{2,1,0:T(8,128)(2,1)} %param.5), calls=%async_computation.1 | async-start | bytes 65536 | tf_op jit(solution)/shard_map/all_to_all | solution.py:29
  25.6 14.8 %all-to-all-start = ((bf16[8,1,8,2176]{3,2,1,0:T(8,128)(2,1)}), bf16[8,1,8,2176]{3,2,1,0:T(8,128)(2,1)S(1)}, u32[]{:S(2)}, u32[]{:S(2)}) async-start(bf16[8,1,8,2176]{3,2,1,0:T(8,128)(2,1)} %bitcast_dynamic-update-slice_fusion), calls=%async_computation | async-start | bytes 557056 | tf_op jit(solution)/shard_map/all_to_all | solution.py:9
  31.6 41.4 %all-reduce.5.cloned.1.call-start = ((), (), s32[]{:S(2)}) async-start(), calls=%async_computation.2 | async-start | bytes 294912 | tf_op jit(solution)/shard_map/psum | solution.py:40
  49.8 70.5 %copy-start.3 = (f32[1,137]{1,0:T(1,128)}, f32[1,137]{1,0:T(1,128)S(1)}, u32[]{:S(2)}) copy-start(f32[1,137]{1,0:T(1,128)S(1)} %psum.15) | copy-start | bytes 1648
  73.9 47.8 %copy-start.1 = (f32[1,137,137]{1,2,0:T(8,128)S(1)}, f32[1,137,137]{1,2,0:T(8,128)}, u32[]{:S(2)}) copy-start(f32[1,137,137]{1,2,0:T(8,128)} %all-reduce.5.cloned.1.call-done) | copy-start | bytes 225232
Sparse Core Ops, SparseCore 0:
  42.9 30.0 all-reduce.4
